TPU v7x, 128 devices: a whole 4x4x4 slice. The times are simulated.
128 devices in a mesh: pairs: 1, cols: 2 (over core), rows: 64 (over z, y, x).
Axes of the slice: x: 4, y: 4, z: 4, core: 2. Of those that a mesh axis runs over, the one named last changes fastest.
Arguments:
- C1: float32 [512, 512], P(('pairs', 'rows'), 'cols')
- C2: float32 [8192, 8192], P(('pairs', 'rows'), 'cols')
- T0: float32 [512, 8192], P(('pairs', 'rows'), 'cols')
- p: float32 [512], P(('pairs', 'rows'))
- q: float32 [8192], P(('pairs', 'cols'))
- eps: float32 [6], P('pairs')
Outputs:
- output 1: float32 [512, 8192], P(('pairs', 'rows'), 'cols')
- output 2: float32 [1], P('pairs')
All inputs are finite; a program needn't handle non-finite values.
Results may differ from a plain program's by a relative error of at most 0.001.
Values are sent between devices in bfloat16 or wider.
A program may use at most 1 GiB of HBM per device.

v0:
```python
import jax
import jax.numpy as jnp
from jax import lax
from jax.sharding import PartitionSpec as P

SWEEPS = 10


def solution(mesh):
    grid_spec = P(("pairs", "rows"), "cols")

    def local_fn(c1_blk, c2_blk, t0_blk, p_blk, q_blk, eps_blk):
        col_pos = lax.axis_index("cols")
        row_pos = lax.axis_index("rows")
        c1_width = c1_blk.shape[1]
        c2_height = c2_blk.shape[0]
        p_full = lax.all_gather(p_blk, "rows", tiled=True)
        q_full = lax.all_gather(q_blk, "cols", tiled=True)
        p_piece = lax.dynamic_slice_in_dim(p_full, col_pos * c1_width, c1_width)
        q_piece = lax.dynamic_slice_in_dim(q_full, row_pos * c2_height, c2_height)
        row_term = lax.psum(jnp.sum(c1_blk * c1_blk * p_piece[None, :], axis=1), "cols")
        col_term = lax.psum(jnp.sum(c2_blk * c2_blk * q_piece[:, None], axis=0), "rows")
        const_blk = row_term[:, None] + col_term[None, :]
        c1_panel = lax.all_gather(c1_blk.astype(jnp.bfloat16), "cols", axis=1, tiled=True)
        c2_panel = lax.all_gather(c2_blk.astype(jnp.bfloat16), "rows", axis=0, tiled=True)

        def cost_of(plan_blk):
            plan_panel = lax.all_gather(plan_blk.astype(jnp.bfloat16), "rows", axis=0, tiled=True)
            lead_blk = jnp.dot(c1_panel, plan_panel, preferred_element_type=jnp.float32)
            lead_panel = lax.all_gather(lead_blk.astype(jnp.bfloat16), "cols", axis=1, tiled=True)
            cross_blk = jnp.dot(lead_panel, c2_panel, preferred_element_type=jnp.float32)
            return const_blk - 2.0 * cross_blk

        def balance(kernel):
            def sweep(sweep_idx, scales):
                row_scale = p_blk / lax.psum(jnp.sum(kernel * scales[1][None, :], axis=1), "cols")
                col_scale = q_blk / lax.psum(jnp.sum(kernel * row_scale[:, None], axis=0), "rows")
                return row_scale, col_scale
            row_scale, col_scale = lax.fori_loop(0, SWEEPS, sweep, (jnp.ones_like(p_blk), jnp.ones_like(q_blk)))
            return row_scale[:, None] * kernel * col_scale[None, :]

        plan_blk = t0_blk
        for step_idx in range(eps_blk.shape[0]):
            cost_blk = cost_of(plan_blk)
            row_shift = lax.pmin(jnp.min(cost_blk, axis=1), "cols")
            kernel = jnp.exp(-(cost_blk - row_shift[:, None]) / eps_blk[step_idx])
            plan_blk = balance(kernel)
        cost_blk = cost_of(plan_blk)
        loss_val = lax.psum(jnp.sum(cost_blk * plan_blk), ("rows", "cols"))
        return plan_blk, loss_val.reshape(1)

    return jax.shard_map(local_fn, mesh=mesh, in_specs=(grid_spec, grid_spec, grid_spec, P(("pairs", "rows")), P(("pairs", "cols")), P("pairs")), out_specs=(grid_spec, P("pairs")), check_vma=False)
```

profile of v0, /device:TPU:1, one launch (start us, length us, event | category | flops | bytes accessed | tf_op | source)
XLA Modules:
  0.0 21716.9 jit_solution(13159797574392842835)
XLA Ops:
  16.9 299.4 %all-reduce.1 = (f32[4096]{0:T(1024)S(1)}, f32[512]{0:T(512)S(1)}) all-reduce(f32[4096]{0:T(1024)S(1)} %get-tuple-element.402, f32[512]{0:T(512)S(1)} %dynamic-update-slice), channel_id=1, replica_groups=mesh['pairs'=1,'cols'=2,'rows'=64] {'rows'}, use_global_device_ids=true, to_apply=%region_3.0 | all-reduce | flops 4608 | bytes 36864 | tf_op jit(solution)/shard_map/psum | solution.py:22
  407.5 3386.9 %while.78 = (s32[]{:T(128)}, f32[8]{0:T(128)}, f32[4096]{0:T(1024)S(1)}, f32[8,4096]{1,0:T(8,128)S(1)}, f32[8]{0:T(128)S(1)}, /*index=5*/f32[4096]{0:T(1024)S(1)}, s32[]{:T(128)}, s32[]{:T(128)}) while((s32[]{:T(128)}, f32[8]{0:T(128)}, f32[4096]{0:T(1024)S(1)}, f32[8,4096]{1,0:T(8,128)S(1)}, f32[8]{0:T(128)S(1)}, ...), condition=%wide.region_11.0_spmd.clone, body=%wide.region_6.0_spmd.clone.sunk | while | flops 139275 | bytes 410083 | solution.py:39
  754.5 286.1 %psum.133 = f32[4096]{0:T(1024)S(1)} all-reduce(f32[4096]{0:T(1024)S(1)} %multiply_reduce_fusion.27), channel_id=1, replica_groups=mesh['pairs'=1,'cols'=2,'rows'=64] {'rows'}, use_global_device_ids=true, to_apply=%region_10.0 | all-reduce | flops 4096 | bytes 32768 | tf_op jit(solution)/shard_map/while/body/eval_jaxpr/psum | solution.py:37
  1098.7 286.1 %psum.133 = f32[4096]{0:T(1024)S(1)} all-reduce(f32[4096]{0:T(1024)S(1)} %multiply_reduce_fusion.27), channel_id=1, replica_groups=mesh['pairs'=1,'cols'=2,'rows'=64] {'rows'}, use_global_device_ids=true, to_apply=%region_10.0 | all-reduce | flops 4096 | bytes 32768 | tf_op jit(solution)/shard_map/while/body/eval_jaxpr/psum | solution.py:37
  1442.9 286.1 %psum.133 = f32[4096]{0:T(1024)S(1)} all-reduce(f32[4096]{0:T(1024)S(1)} %multiply_reduce_fusion.27), channel_id=1, replica_groups=mesh['pairs'=1,'cols'=2,'rows'=64] {'rows'}, use_global_device_ids=true, to_apply=%region_10.0 | all-reduce | flops 4096 | bytes 32768 | tf_op jit(solution)/shard_map/while/body/eval_jaxpr/psum | solution.py:37
  1787.2 286.1 %psum.133 = f32[4096]{0:T(1024)S(1)} all-reduce(f32[4096]{0:T(1024)S(1)} %multiply_reduce_fusion.27), channel_id=1, replica_groups=mesh['pairs'=1,'cols'=2,'rows'=64] {'rows'}, use_global_device_ids=true, to_apply=%region_10.0 | all-reduce | flops 4096 | bytes 32768 | tf_op jit(solution)/shard_map/while/body/eval_jaxpr/psum | solution.py:37
  2131.4 286.1 %psum.133 = f32[4096]{0:T(1024)S(1)} all-reduce(f32[4096]{0:T(1024)S(1)} %multiply_reduce_fusion.27), channel_id=1, replica_groups=mesh['pairs'=1,'cols'=2,'rows'=64] {'rows'}, use_global_device_ids=true, to_apply=%region_10.0 | all-reduce | flops 4096 | bytes 32768 | tf_op jit(solution)/shard_map/while/body/eval_jaxpr/psum | solution.py:37
  3508.3 286.1 %psum.133 = f32[4096]{0:T(1024)S(1)} all-reduce(f32[4096]{0:T(1024)S(1)} %multiply_reduce_fusion.27), channel_id=1, replica_groups=mesh['pairs'=1,'cols'=2,'rows'=64] {'rows'}, use_global_device_ids=true, to_apply=%region_10.0 | all-reduce | flops 4096 | bytes 32768 | tf_op jit(solution)/shard_map/while/body/eval_jaxpr/psum | solution.py:37
  3945.0 3390.4 %while.79 = (s32[]{:T(128)}, f32[8]{0:T(128)}, f32[4096]{0:T(1024)S(1)}, f32[8,4096]{1,0:T(8,128)S(1)}, f32[8]{0:T(128)S(1)}, /*index=5*/f32[4096]{0:T(1024)S(1)}, s32[]{:T(128)}, s32[]{:T(128)}) while((s32[]{:T(128)}, f32[8]{0:T(128)}, f32[4096]{0:T(1024)S(1)}, f32[8,4096]{1,0:T(8,128)S(1)}, f32[8]{0:T(128)S(1)}, ...), condition=%wide.region_19.0_spmd.clone, body=%wide.region_14.0_spmd.clone.sunk | while | flops 139275 | bytes 410083 | solution.py:39
  3947.7 290.1 %psum.135 = f32[4096]{0:T(1024)S(1)} all-reduce(f32[4096]{0:T(1024)S(1)} %multiply_reduce_fusion.29), channel_id=1, replica_groups=mesh['pairs'=1,'cols'=2,'rows'=64] {'rows'}, use_global_device_ids=true, to_apply=%region_18.0 | all-reduce | flops 4096 | bytes 32768 | tf_op jit(solution)/shard_map/while/body/eval_jaxpr/psum | solution.py:37
  4984.0 286.1 %psum.135 = f32[4096]{0:T(1024)S(1)} all-reduce(f32[4096]{0:T(1024)S(1)} %multiply_reduce_fusion.29), channel_id=1, replica_groups=mesh['pairs'=1,'cols'=2,'rows'=64] {'rows'}, use_global_device_ids=true, to_apply=%region_18.0 | all-reduce | flops 4096 | bytes 32768 | tf_op jit(solution)/shard_map/while/body/eval_jaxpr/psum | solution.py:37
  6360.9 286.1 %psum.135 = f32[4096]{0:T(1024)S(1)} all-reduce(f32[4096]{0:T(1024)S(1)} %multiply_reduce_fusion.29), channel_id=1, replica_groups=mesh['pairs'=1,'cols'=2,'rows'=64] {'rows'}, use_global_device_ids=true, to_apply=%region_18.0 | all-reduce | flops 4096 | bytes 32768 | tf_op jit(solution)/shard_map/while/body/eval_jaxpr/psum | solution.py:37
  6705.1 286.1 %psum.135 = f32[4096]{0:T(1024)S(1)} all-reduce(f32[4096]{0:T(1024)S(1)} %multiply_reduce_fusion.29), channel_id=1, replica_groups=mesh['pairs'=1,'cols'=2,'rows'=64] {'rows'}, use_global_device_ids=true, to_apply=%region_18.0 | all-reduce | flops 4096 | bytes 32768 | tf_op jit(solution)/shard_map/while/body/eval_jaxpr/psum | solution.py:37
  7486.2 3390.4 %while.80 = (s32[]{:T(128)}, f32[8]{0:T(128)}, f32[4096]{0:T(1024)S(1)}, f32[8,4096]{1,0:T(8,128)S(1)}, f32[8]{0:T(128)S(1)}, /*index=5*/f32[4096]{0:T(1024)S(1)}, s32[]{:T(128)}, s32[]{:T(128)}) while((s32[]{:T(128)}, f32[8]{0:T(128)}, f32[4096]{0:T(1024)S(1)}, f32[8,4096]{1,0:T(8,128)S(1)}, f32[8]{0:T(128)S(1)}, ...), condition=%wide.region_27.0_spmd.clone, body=%wide.region_22.0_spmd.clone.sunk | while | flops 139275 | bytes 410083 | solution.py:39
  7489.0 290.1 %psum.137 = f32[4096]{0:T(1024)S(1)} all-reduce(f32[4096]{0:T(1024)S(1)} %multiply_reduce_fusion.31), channel_id=1, replica_groups=mesh['pairs'=1,'cols'=2,'rows'=64] {'rows'}, use_global_device_ids=true, to_apply=%region_26.0 | all-reduce | flops 4096 | bytes 32768 | tf_op jit(solution)/shard_map/while/body/eval_jaxpr/psum | solution.py:37
  7836.7 286.1 %psum.137 = f32[4096]{0:T(1024)S(1)} all-reduce(f32[4096]{0:T(1024)S(1)} %multiply_reduce_fusion.31), channel_id=1, replica_groups=mesh['pairs'=1,'cols'=2,'rows'=64] {'rows'}, use_global_device_ids=true, to_apply=%region_26.0 | all-reduce | flops 4096 | bytes 32768 | tf_op jit(solution)/shard_map/while/body/eval_jaxpr/psum | solution.py:37
  9557.9 286.1 %psum.137 = f32[4096]{0:T(1024)S(1)} all-reduce(f32[4096]{0:T(1024)S(1)} %multiply_reduce_fusion.31), channel_id=1, replica_groups=mesh['pairs'=1,'cols'=2,'rows'=64] {'rows'}, use_global_device_ids=true, to_apply=%region_26.0 | all-reduce | flops 4096 | bytes 32768 | tf_op jit(solution)/shard_map/while/body/eval_jaxpr/psum | solution.py:37
  11027.2 3390.4 %while.81 = (s32[]{:T(128)}, f32[8]{0:T(128)}, f32[4096]{0:T(1024)S(1)}, f32[8,4096]{1,0:T(8,128)S(1)}, f32[8]{0:T(128)S(1)}, /*index=5*/f32[4096]{0:T(1024)S(1)}, s32[]{:T(128)}, s32[]{:T(128)}) while((s32[]{:T(128)}, f32[8]{0:T(128)}, f32[4096]{0:T(1024)S(1)}, f32[8,4096]{1,0:T(8,128)S(1)}, f32[8]{0:T(128)S(1)}, ...), condition=%wide.region_35.0_spmd.clone, body=%wide.region_30.0_spmd.clone.sunk | while | flops 139275 | bytes 410083 | solution.py:39
  11030.0 290.1 %psum.139 = f32[4096]{0:T(1024)S(1)} all-reduce(f32[4096]{0:T(1024)S(1)} %multiply_reduce_fusion.33), channel_id=1, replica_groups=mesh['pairs'=1,'cols'=2,'rows'=64] {'rows'}, use_global_device_ids=true, to_apply=%region_34.0 | all-reduce | flops 4096 | bytes 32768 | tf_op jit(solution)/shard_map/while/body/eval_jaxpr/psum | solution.py:37
  12754.6 286.1 %psum.139 = f32[4096]{0:T(1024)S(1)} all-reduce(f32[4096]{0:T(1024)S(1)} %multiply_reduce_fusion.33), channel_id=1, replica_groups=mesh['pairs'=1,'cols'=2,'rows'=64] {'rows'}, use_global_device_ids=true, to_apply=%region_34.0 | all-reduce | flops 4096 | bytes 32768 | tf_op jit(solution)/shard_map/while/body/eval_jaxpr/psum | solution.py:37
  14131.6 286.1 %psum.139 = f32[4096]{0:T(1024)S(1)} all-reduce(f32[4096]{0:T(1024)S(1)} %multiply_reduce_fusion.33), channel_id=1, replica_groups=mesh['pairs'=1,'cols'=2,'rows'=64] {'rows'}, use_global_device_ids=true, to_apply=%region_34.0 | all-reduce | flops 4096 | bytes 32768 | tf_op jit(solution)/shard_map/while/body/eval_jaxpr/psum | solution.py:37
  14568.1 3390.4 %while.82 = (s32[]{:T(128)}, f32[8]{0:T(128)}, f32[4096]{0:T(1024)S(1)}, f32[8,4096]{1,0:T(8,128)S(1)}, f32[8]{0:T(128)S(1)}, /*index=5*/f32[4096]{0:T(1024)S(1)}, s32[]{:T(128)}, s32[]{:T(128)}) while((s32[]{:T(128)}, f32[8]{0:T(128)}, f32[4096]{0:T(1024)S(1)}, f32[8,4096]{1,0:T(8,128)S(1)}, f32[8]{0:T(128)S(1)}, ...), condition=%wide.region_43.0_spmd.clone, body=%wide.region_38.0_spmd.clone.sunk | while | flops 139275 | bytes 410083 | solution.py:39
  14570.9 290.1 %psum.141 = f32[4096]{0:T(1024)S(1)} all-reduce(f32[4096]{0:T(1024)S(1)} %multiply_reduce_fusion.35), channel_id=1, replica_groups=mesh['pairs'=1,'cols'=2,'rows'=64] {'rows'}, use_global_device_ids=true, to_apply=%region_42.0 | all-reduce | flops 4096 | bytes 32768 | tf_op jit(solution)/shard_map/while/body/eval_jaxpr/psum | solution.py:37
  14918.6 286.1 %psum.141 = f32[4096]{0:T(1024)S(1)} all-reduce(f32[4096]{0:T(1024)S(1)} %multiply_reduce_fusion.35), channel_id=1, replica_groups=mesh['pairs'=1,'cols'=2,'rows'=64] {'rows'}, use_global_device_ids=true, to_apply=%region_42.0 | all-reduce | flops 4096 | bytes 32768 | tf_op jit(solution)/shard_map/while/body/eval_jaxpr/psum | solution.py:37
  16295.6 286.1 %psum.141 = f32[4096]{0:T(1024)S(1)} all-reduce(f32[4096]{0:T(1024)S(1)} %multiply_reduce_fusion.35), channel_id=1, replica_groups=mesh['pairs'=1,'cols'=2,'rows'=64] {'rows'}, use_global_device_ids=true, to_apply=%region_42.0 | all-reduce | flops 4096 | bytes 32768 | tf_op jit(solution)/shard_map/while/body/eval_jaxpr/psum | solution.py:37
  16639.8 286.1 %psum.141 = f32[4096]{0:T(1024)S(1)} all-reduce(f32[4096]{0:T(1024)S(1)} %multiply_reduce_fusion.35), channel_id=1, replica_groups=mesh['pairs'=1,'cols'=2,'rows'=64] {'rows'}, use_global_device_ids=true, to_apply=%region_42.0 | all-reduce | flops 4096 | bytes 32768 | tf_op jit(solution)/shard_map/while/body/eval_jaxpr/psum | solution.py:37
  18109.3 3390.4 %while.83 = (s32[]{:T(128)}, f32[8]{0:T(128)}, f32[4096]{0:T(1024)S(1)}, f32[8,4096]{1,0:T(8,128)S(1)}, f32[8]{0:T(128)S(1)}, /*index=5*/f32[4096]{0:T(1024)S(1)}, s32[]{:T(128)}, s32[]{:T(128)}) while((s32[]{:T(128)}, f32[8]{0:T(128)}, f32[4096]{0:T(1024)S(1)}, f32[8,4096]{1,0:T(8,128)S(1)}, f32[8]{0:T(128)S(1)}, ...), condition=%wide.region_51.0_spmd.clone, body=%wide.region_46.0_spmd.clone.sunk | while | flops 139275 | bytes 410083 | solution.py:39
  18112.1 290.1 %psum.143 = f32[4096]{0:T(1024)S(1)} all-reduce(f32[4096]{0:T(1024)S(1)} %multiply_reduce_fusion.37), channel_id=1, replica_groups=mesh['pairs'=1,'cols'=2,'rows'=64] {'rows'}, use_global_device_ids=true, to_apply=%region_50.0 | all-reduce | flops 4096 | bytes 32768 | tf_op jit(solution)/shard_map/while/body/eval_jaxpr/psum | solution.py:37
  18459.8 286.1 %psum.143 = f32[4096]{0:T(1024)S(1)} all-reduce(f32[4096]{0:T(1024)S(1)} %multiply_reduce_fusion.37), channel_id=1, replica_groups=mesh['pairs'=1,'cols'=2,'rows'=64] {'rows'}, use_global_device_ids=true, to_apply=%region_50.0 | all-reduce | flops 4096 | bytes 32768 | tf_op jit(solution)/shard_map/while/body/eval_jaxpr/psum | solution.py:37
  18804.1 286.1 %psum.143 = f32[4096]{0:T(1024)S(1)} all-reduce(f32[4096]{0:T(1024)S(1)} %multiply_reduce_fusion.37), channel_id=1, replica_groups=mesh['pairs'=1,'cols'=2,'rows'=64] {'rows'}, use_global_device_ids=true, to_apply=%region_50.0 | all-reduce | flops 4096 | bytes 32768 | tf_op jit(solution)/shard_map/while/body/eval_jaxpr/psum | solution.py:37
  20181.0 286.1 %psum.143 = f32[4096]{0:T(1024)S(1)} all-reduce(f32[4096]{0:T(1024)S(1)} %multiply_reduce_fusion.37), channel_id=1, replica_groups=mesh['pairs'=1,'cols'=2,'rows'=64] {'rows'}, use_global_device_ids=true, to_apply=%region_50.0 | all-reduce | flops 4096 | bytes 32768 | tf_op jit(solution)/shard_map/while/body/eval_jaxpr/psum | solution.py:37
  20525.2 286.1 %psum.143 = f32[4096]{0:T(1024)S(1)} all-reduce(f32[4096]{0:T(1024)S(1)} %multiply_reduce_fusion.37), channel_id=1, replica_groups=mesh['pairs'=1,'cols'=2,'rows'=64] {'rows'}, use_global_device_ids=true, to_apply=%region_50.0 | all-reduce | flops 4096 | bytes 32768 | tf_op jit(solution)/shard_map/while/body/eval_jaxpr/psum | solution.py:37
  (615 shorter events, 14228.8 us)
Async XLA Ops:
  7.2 309.2 %copy-start.9 = (f32[8,256]{1,0:T(8,128)S(1)}, f32[8,256]{1,0:T(8,128)}, u32[]{:S(2)}) copy-start(f32[8,256]{1,0:T(8,128)} %param.18) | copy-start | bytes 24580
  7.2 368.4 %copy-start.8 = (f32[6]{0:T(128)S(1)}, f32[6]{0:T(128)}, u32[]{:S(2)}) copy-start(f32[6]{0:T(128)} %param.23) | copy-start | bytes 76
  7.2 369.1 %all-gather.9.cloned.1.call-start = ((), (), s32[]{:S(2)}) async-start(), calls=%async_computation | async-start | bytes 4259840 | tf_op jit(solution)/shard_map/all_gather | solution.py:28
  8.8 372.2 %all-gather.11.cloned.1.call-start = ((), (), s32[]{:S(2)}) async-start(), calls=%async_computation.1 | async-start | bytes 68157440 | tf_op jit(solution)/shard_map/all_gather | solution.py:25
  15.4 3896.0 %all-gather.13.cloned.1.call-start = ((), (), s32[]{:S(2)}) async-start(), calls=%async_computation.2 | async-start | bytes 4259840 | tf_op jit(solution)/shard_map/all_gather | solution.py:28
  754.4 286.2 %copy-start.3 = (f32[8]{0:T(128)}, f32[8]{0:T(128)S(1)}, u32[]{:S(2)}) copy-start(f32[8]{0:T(128)S(1)} %div.144) | copy-start | bytes 100 | tf_op jit(solution)/shard_map/while
  1098.6 286.2 %copy-start.3 = (f32[8]{0:T(128)}, f32[8]{0:T(128)S(1)}, u32[]{:S(2)}) copy-start(f32[8]{0:T(128)S(1)} %div.144) | copy-start | bytes 100 | tf_op jit(solution)/shard_map/while
  1787.1 286.2 %copy-start.3 = (f32[8]{0:T(128)}, f32[8]{0:T(128)S(1)}, u32[]{:S(2)}) copy-start(f32[8]{0:T(128)S(1)} %div.144) | copy-start | bytes 100 | tf_op jit(solution)/shard_map/while
  2131.3 286.2 %copy-start.3 = (f32[8]{0:T(128)}, f32[8]{0:T(128)S(1)}, u32[]{:S(2)}) copy-start(f32[8]{0:T(128)S(1)} %div.144) | copy-start | bytes 100 | tf_op jit(solution)/shard_map/while
  2475.5 286.2 %copy-start.3 = (f32[8]{0:T(128)}, f32[8]{0:T(128)S(1)}, u32[]{:S(2)}) copy-start(f32[8]{0:T(128)S(1)} %div.144) | copy-start | bytes 100 | tf_op jit(solution)/shard_map/while
  2819.8 286.2 %copy-start.3 = (f32[8]{0:T(128)}, f32[8]{0:T(128)S(1)}, u32[]{:S(2)}) copy-start(f32[8]{0:T(128)S(1)} %div.144) | copy-start | bytes 100 | tf_op jit(solution)/shard_map/while
  3508.2 286.2 %copy-start.3 = (f32[8]{0:T(128)}, f32[8]{0:T(128)S(1)}, u32[]{:S(2)}) copy-start(f32[8]{0:T(128)S(1)} %div.144) | copy-start | bytes 100 | tf_op jit(solution)/shard_map/while
  3796.4 3656.0 %all-gather.15.cloned.1.call-start = ((), (), s32[]{:S(2)}) async-start(), calls=%async_computation.3 | async-start | bytes 4259840 | tf_op jit(solution)/shard_map/all_gather | solution.py:28
  3947.6 290.2 %copy-start.4 = (f32[8]{0:T(128)}, f32[8]{0:T(128)S(1)}, u32[]{:S(2)}) copy-start(f32[8]{0:T(128)S(1)} %div.146) | copy-start | bytes 100 | tf_op jit(solution)/shard_map/while
  4295.4 286.2 %copy-start.4 = (f32[8]{0:T(128)}, f32[8]{0:T(128)S(1)}, u32[]{:S(2)}) copy-start(f32[8]{0:T(128)S(1)} %div.146) | copy-start | bytes 100 | tf_op jit(solution)/shard_map/while
  4983.8 286.2 %copy-start.4 = (f32[8]{0:T(128)}, f32[8]{0:T(128)S(1)}, u32[]{:S(2)}) copy-start(f32[8]{0:T(128)S(1)} %div.146) | copy-start | bytes 100 | tf_op jit(solution)/shard_map/while
  5328.1 286.2 %copy-start.4 = (f32[8]{0:T(128)}, f32[8]{0:T(128)S(1)}, u32[]{:S(2)}) copy-start(f32[8]{0:T(128)S(1)} %div.146) | copy-start | bytes 100 | tf_op jit(solution)/shard_map/while
  5672.3 286.2 %copy-start.4 = (f32[8]{0:T(128)}, f32[8]{0:T(128)S(1)}, u32[]{:S(2)}) copy-start(f32[8]{0:T(128)S(1)} %div.146) | copy-start | bytes 100 | tf_op jit(solution)/shard_map/while
  6360.8 286.2 %copy-start.4 = (f32[8]{0:T(128)}, f32[8]{0:T(128)S(1)}, u32[]{:S(2)}) copy-start(f32[8]{0:T(128)S(1)} %div.146) | copy-start | bytes 100 | tf_op jit(solution)/shard_map/while
  6705.0 286.2 %copy-start.4 = (f32[8]{0:T(128)}, f32[8]{0:T(128)S(1)}, u32[]{:S(2)}) copy-start(f32[8]{0:T(128)S(1)} %div.146) | copy-start | bytes 100 | tf_op jit(solution)/shard_map/while
  7049.2 286.2 %copy-start.4 = (f32[8]{0:T(128)}, f32[8]{0:T(128)S(1)}, u32[]{:S(2)}) copy-start(f32[8]{0:T(128)S(1)} %div.146) | copy-start | bytes 100 | tf_op jit(solution)/shard_map/while
  7337.4 3656.3 %all-gather.17.cloned.1.call-start = ((), (), s32[]{:S(2)}) async-start(), calls=%async_computation.4 | async-start | bytes 4259840 | tf_op jit(solution)/shard_map/all_gather | solution.py:28
  7488.9 290.2 %copy-start.5 = (f32[8]{0:T(128)}, f32[8]{0:T(128)S(1)}, u32[]{:S(2)}) copy-start(f32[8]{0:T(128)S(1)} %div.148) | copy-start | bytes 100 | tf_op jit(solution)/shard_map/while
  7836.6 286.2 %copy-start.5 = (f32[8]{0:T(128)}, f32[8]{0:T(128)S(1)}, u32[]{:S(2)}) copy-start(f32[8]{0:T(128)S(1)} %div.148) | copy-start | bytes 100 | tf_op jit(solution)/shard_map/while
  8180.8 286.2 %copy-start.5 = (f32[8]{0:T(128)}, f32[8]{0:T(128)S(1)}, u32[]{:S(2)}) copy-start(f32[8]{0:T(128)S(1)} %div.148) | copy-start | bytes 100 | tf_op jit(solution)/shard_map/while
  8525.1 286.2 %copy-start.5 = (f32[8]{0:T(128)}, f32[8]{0:T(128)S(1)}, u32[]{:S(2)}) copy-start(f32[8]{0:T(128)S(1)} %div.148) | copy-start | bytes 100 | tf_op jit(solution)/shard_map/while
  10878.7 3655.8 %all-gather.19.cloned.1.call-start = ((), (), s32[]{:S(2)}) async-start(), calls=%async_computation.5 | async-start | bytes 4259840 | tf_op jit(solution)/shard_map/all_gather | solution.py:28
  11029.9 290.2 %copy-start.6 = (f32[8]{0:T(128)}, f32[8]{0:T(128)S(1)}, u32[]{:S(2)}) copy-start(f32[8]{0:T(128)S(1)} %div.150) | copy-start | bytes 100 | tf_op jit(solution)/shard_map/while
  14419.6 3655.9 %all-gather.21.cloned.1.call-start = ((), (), s32[]{:S(2)}) async-start(), calls=%async_computation.6 | async-start | bytes 4259840 | tf_op jit(solution)/shard_map/all_gather | solution.py:28
  14570.8 290.2 %copy-start.7 = (f32[8]{0:T(128)}, f32[8]{0:T(128)S(1)}, u32[]{:S(2)}) copy-start(f32[8]{0:T(128)S(1)} %div.152) | copy-start | bytes 100 | tf_op jit(solution)/shard_map/while
  17960.5 3656.2 %all-gather.23.cloned.1.call-start = ((), (), s32[]{:S(2)}) async-start(), calls=%async_computation.7 | async-start | bytes 4259840 | tf_op jit(solution)/shard_map/all_gather | solution.py:28
  18112.0 290.2 %copy-start.2 = (f32[8]{0:T(128)}, f32[8]{0:T(128)S(1)}, u32[]{:S(2)}) copy-start(f32[8]{0:T(128)S(1)} %div.154) | copy-start | bytes 100 | tf_op jit(solution)/shard_map/while
  (42 other events, 11064.7 us)
Sparse Core Ops, SparseCore 0:
  11.5 70.0 all-gather.8
  84.4 278.5 all-gather.10
  3796.5 114.8 all-gather.12
  7337.5 114.8 all-gather.14
  10878.8 114.8 all-gather.16
  14419.7 114.8 all-gather.18
  17960.7 114.8 all-gather.20
  21501.9 114.8 all-gather.22
where the time goes:
time: 21700 us
  blocking collectives  20800 us (96%)
  waiting for transfers between devices  690 us (3%)
    psum x60, blocking collectives, sweep(): lax.psum(jnp.sum(kernel * row_scale[:, None], axis=0), 'rows')  17200 us
    psum x60, blocking collectives, sweep(): lax.psum(jnp.sum(kernel * scales[1][None, :], axis=1), 'cols')  3140 us
    all_gather x7, waiting for transfers between devices, cost_of(): lax.all_gather(plan_blk.astype(jnp.bfloat16), 'rows', axis=0, tiled=True)  690 us
  transfers between devices with their start and end apart: 8, of which 6 were waited for; matrix products, arithmetic and copies ran while one was open for 0% of the time, Pallas kernels for 0%

commit v1 on v0

v1 whole, which is shorter than its diff:
```python
import heapq
import itertools
import math

import jax
import jax.numpy as jnp
from jax import lax
from jax.experimental import pallas as pl
from jax.experimental.pallas import tpu as pltpu
from jax.sharding import PartitionSpec as P

SWEEPS = 10
MESH = pl.DeviceIdType.MESH
JB = 64
JT = JB // 8
F32, BF16 = jnp.float32, jnp.bfloat16
ORDERS = ((0, 1, 2), (1, 2, 0), (2, 0, 1))


def torus_of(chips):
    return {64: (4, 4, 4), 8: (4, 2, 1), 16: (4, 4, 1)}[chips]


def split3(n):
    cuts = [0, (n + 2) // 3, (2 * n + 2) // 3, n]
    return [(cuts[k], cuts[k + 1]) for k in range(3)]


def tree_plan(dims, tiles, tile_us, lat_us=2.0):
    rings = {1: (), 2: ((1, "f", 1),), 4: ((1, "f", 1), (3, "f", -1), (2, "a", 1), (2, "b", -1))}
    msgs = []
    for color, order in enumerate(ORDERS):
        lo, hi = split3(tiles)[color]
        mid = lo + (hi - lo + 1) // 2
        for dst in itertools.product(*(range(n) for n in dims)):
            used = [k for k in range(3) if dst[order[k]]]
            if not used or lo == hi:
                continue
            d = order[used[-1]]
            for at, part, sign in rings[dims[d]]:
                a, b = {"f": (lo, hi), "a": (lo, mid), "b": (mid, hi)}[part]
                if at != dst[d] or a == b:
                    continue
                src = list(dst)
                src[d] = (src[d] - sign) % dims[d]
                msgs.append(dict(id=len(msgs), color=color, src=tuple(src), dst=dst, link=(d, sign), lo=a, hi=b))
    into = {}
    for m in msgs:
        into.setdefault((m["color"], m["dst"]), []).append(m)
    users = {m["id"]: [] for m in msgs}
    for m in msgs:
        m["deps"] = [
            e["id"] for e in into.get((m["color"], m["src"]), []) if e["lo"] < m["hi"] and m["lo"] < e["hi"]
        ]
        for e in m["deps"]:
            users[e].append(m)
    depth = {}

    def depth_of(m):
        if m["id"] not in depth:
            depth[m["id"]] = 1 + max([depth_of(u) for u in users[m["id"]]], default=0)
        return depth[m["id"]]

    ops, free, arrivals, missing = [], {}, [], {m["id"]: len(m["deps"]) for m in msgs}
    left = {}
    for m in msgs:
        left[m["dst"]] = left.get(m["dst"], 0) + 1

    def send(ready, now):
        for m in sorted(ready, key=lambda m: (-depth_of(m), m["color"], m["id"])):
            ops.append(("send", m))
            end = max(now, free.get(m["link"], 0.0)) + (m["hi"] - m["lo"]) * tile_us
            free[m["link"]] = end
            heapq.heappush(arrivals, (end + lat_us, m["id"]))

    send([m for m in msgs if not m["deps"]], 0.0)
    now = 0.0
    while arrivals:
        now, k = heapq.heappop(arrivals)
        m = msgs[k]
        ops.append(("wait", m))
        ready = []
        for u in users[k]:
            missing[u["id"]] -= 1
            if not missing[u["id"]]:
                ready.append(u)
        send(ready, now)
        left[m["dst"]] -= 1
        if not left[m["dst"]]:
            ops.append(("slot", m["dst"]))
    links = sorted({m["link"] for m in msgs})
    totals = {k: sum(m["hi"] - m["lo"] for m in msgs if m["link"] == k) for k in links}
    return dict(msgs=msgs, ops=ops, links=links, totals=totals, end=now)


def make_kernel(dims, n_rows, n_cols, steps, sweeps):
    X, Y, Z = dims
    CH = X * Y * Z
    NR = n_rows // CH
    G = NR // 8
    NT = n_rows // 128
    TB = JT * NT
    HB = CH // 2
    JN = n_cols // 2 // 128
    JW = JN // 2
    NT0 = G * JW
    TT0 = NT0 + 2 * G
    KJ = CH * JB
    CK = min(512, KJ)
    GS = min(8, CH // 2)
    NG = CH // GS
    assert NT == 4 and n_cols == CH * 128 and JN == HB
    plan0 = tree_plan(dims, TT0, 4096 / 46.6e3)
    plan = tree_plan(dims, TB, 4096 / 46.6e3)
    links = plan["links"]
    NL = len(links)
    peers = [(d, k) for d in range(3) for k in range(1, dims[d])]
    strides = (1, X, X * Y)

    def slot_of(offset):
        return offset[0] + X * offset[1] + X * Y * offset[2]

    def kernel(
        eps_ref, p_ref, c1_ref, c2_ref, t0_ref, q_ref,
        out_ref, loss_ref,
        land, kbuf, g0, tt, c1f, c1b, c2n, c2p, bacc, lp, lprecv, bp, qf, qrep, vbuf, cbuf,
        mb, sb, fb, ub, ap, xs, xr, mss, msr, pv, ars, arr, arps, arpr, obuf, orecv, trb,
        send_sem, recv_sem, credit, x_ssem, x_rsem, ms_sem, lp_sem, c1_sem, c2_sem, q_sem, ar_ssem, ar_rsem, arp_sem, o_sem,
    ):
        chip = lax.axis_index("rows")
        core = lax.axis_index("cols")
        other = 1 - core
        pos = (lax.rem(chip, X), lax.rem(lax.div(chip, X), Y), lax.div(chip, X * Y))

        def moved(d, k):
            return chip + (lax.rem(pos[d] + k + dims[d], dims[d]) - pos[d]) * strides[d]

        near = {link: moved(*link) for link in links}

        def source_of(slot):
            off = (lax.rem(slot, X), lax.rem(lax.div(slot, X), Y), lax.div(slot, X * Y))
            at = [lax.rem(pos[d] + dims[d] - off[d], dims[d]) for d in range(3)]
            return at[0] + X * at[1] + X * Y * at[2]

        def to_partner(src, dst, ssem, rsem):
            return pltpu.make_async_remote_copy(
                src_ref=src, dst_ref=dst, send_sem=ssem, recv_sem=rsem,
                device_id={"cols": other}, device_id_type=MESH,
            )

        def tree_copy(buf, width, m):
            n = m["hi"] - m["lo"]
            return pltpu.make_async_remote_copy(
                src_ref=buf.at[pl.ds(slot_of(m["src"]) * width + m["lo"], n)],
                dst_ref=buf.at[pl.ds(slot_of(m["dst"]) * width + m["lo"], n)],
                send_sem=send_sem.at[links.index(m["link"])],
                recv_sem=recv_sem.at[m["id"]],
                device_id={"rows": near[m["link"]]},
                device_id_type=MESH,
            )

        def tree(buf, width, the_plan, before_send=None, on_slot=None, fillers=()):
            fillers, ready, sends = list(fillers), [], 0
            for op, m in the_plan["ops"]:
                if op == "send":
                    if before_send is not None:
                        before_send(m)
                    tree_copy(buf, width, m).start()
                elif op == "wait":
                    tree_copy(buf, width, m).wait_recv()
                    sends += 1
                    if ready:
                        on_slot(ready.pop(0))
                    elif fillers and sends >= fillers[0][0]:
                        fillers.pop(0)[1]()
                elif on_slot is not None:
                    ready.append(slot_of(m))
            for s in ready:
                on_slot(s)
            for _, f in fillers:
                f()

        def tree_sent(buf, the_plan):
            for k, link in enumerate(links):
                n = the_plan["totals"][link]
                ref = buf.at[pl.ds(0, n)]
                pltpu.make_async_copy(ref, ref, send_sem.at[k]).wait()

        def give_credit():
            for d, sign in links:
                pl.semaphore_signal(credit, inc=1, device_id={"rows": moved(d, -sign)}, device_id_type=MESH)

        def all_sum_send(use, stage):
            for n, k in enumerate(range(1, dims[stage])):
                pltpu.make_async_remote_copy(
                    src_ref=ars.at[use, stage], dst_ref=arr.at[use, stage, n],
                    send_sem=ar_ssem.at[use, stage, n], recv_sem=ar_rsem.at[use, stage, n],
                    device_id={"rows": moved(stage, k)}, device_id_type=MESH,
                ).start()

        def all_sum_get(use, stage):
            total = ars[use, stage]
            for n, k in enumerate(range(1, dims[stage])):
                pltpu.make_async_remote_copy(
                    src_ref=ars.at[use, stage], dst_ref=arr.at[use, stage, n],
                    send_sem=ar_ssem.at[use, stage, n], recv_sem=ar_rsem.at[use, stage, n],
                    device_id={"rows": moved(stage, k)}, device_id_type=MESH,
                ).wait()
                total = total + arr[use, stage, n]
            return total

        def all_sum_step(use, stage):
            total = all_sum_get(use, stage)
            if stage < 2:
                ars[use, stage + 1] = total
                all_sum_send(use, stage + 1)
            else:
                arps[use] = total
                to_partner(arps.at[use], arpr.at[use], arp_sem.at[use, 0], arp_sem.at[use, 1]).start()

        barrier = pltpu.get_barrier_semaphore()
        for d, k in peers:
            pl.semaphore_signal(barrier, inc=1, device_id={"rows": moved(d, k)}, device_id_type=MESH)
        pl.semaphore_signal(barrier, inc=1, device_id={"cols": other}, device_id_type=MESH)

        row = lax.broadcasted_iota(jnp.int32, (8, 128), 0)
        lane = lax.broadcasted_iota(jnp.int32, (8, 128), 1)

        for g in range(G):
            rows = slice(g * 8, g * 8 + 8)
            pair = jnp.concatenate([c1_ref[rows, :128], c1_ref[rows, 128:]], axis=0)
            g0[NT0 + core * G + g] = pair.astype(BF16)
        c1_copy = to_partner(
            g0.at[pl.ds(NT0 + core * G, G)], g0.at[pl.ds(NT0 + core * G, G)], c1_sem.at[0], c1_sem.at[1]
        )
        q_copy = to_partner(q_ref, qf.at[pl.ds(core * HB, HB)], q_sem.at[0], q_sem.at[1])

        tile = jnp.zeros((8, 128), F32)
        for t in range(2):
            part = jnp.zeros((1, 128), F32)
            for k in range(NR):
                entry = c1_ref[k : k + 1, t * 128 : t * 128 + 128]
                part = part + entry * entry * p_ref[k]
            tile = jnp.where(row == 2 * core + t, jnp.broadcast_to(part, (8, 128)), tile)
        where = (row - 4) * 128 + lane
        for k in range(NR):
            tile = jnp.where(where == chip * NR + k, p_ref[k], tile)
        ars[0, 0] = tile
        for g in range(G):
            rows = slice(g * 8, g * 8 + 8)
            for t in range(JW):
                a, b = t0_ref[rows, 256 * t : 256 * t + 128], t0_ref[rows, 256 * t + 128 : 256 * t + 256]
                g0[g * JW + t] = jnp.concatenate([a, b], axis=0).astype(BF16)
        qf[pl.ds(core * HB, HB)] = q_ref[...]

        pl.semaphore_wait(barrier, len(peers) + 1)
        give_credit()
        c1_copy.start()
        q_copy.start()
        all_sum_send(0, 0)

        c2_copy = to_partner(c2n.at[pl.ds(core * HB, HB)], c2n.at[pl.ds(core * HB, HB)], c2_sem.at[0], c2_sem.at[1])
        bp[...] = jnp.zeros_like(bp)

        def round_c2(first, last):
            for t in range(first, last):
                blk = c2_ref[:, t * 128 : t * 128 + 128]
                c2n[core * HB + t] = blk.astype(BF16)
                bp[...] += blk * blk * q_ref[t : t + 1, :]

        def finish_b():
            bp[...] = jnp.broadcast_to(jnp.sum(bp[...], axis=1, keepdims=True), (128, 128))

        src = lax.broadcasted_iota(jnp.int32, (128, 128), 0)
        dst = lax.broadcasted_iota(jnp.int32, (128, 128), 1)
        picks = [
            jnp.where((src - core * JB == dst - h * JB) & (dst >= h * JB) & (dst < h * JB + JB), 1.0, 0.0).astype(BF16)
            for h in range(2)
        ]

        def order_c2(first, last):
            for t in range(first, last):
                a = jnp.dot(c2n[source_of(2 * t)], picks[0], preferred_element_type=F32)
                b = jnp.dot(c2n[source_of(2 * t + 1)], picks[1], preferred_element_type=F32)
                c2p[:, t * 128 : t * 128 + 128] = (a + b).astype(BF16)

        def order_q(first, last):
            def one(s, carry):
                line = jnp.broadcast_to(qf[pl.ds(source_of(s), 1), :], (8, 128))
                for jt in range(JT):
                    own = jnp.where(lane == core * JB + jt * 8 + row, line, 0.0)
                    qrep[s, jt] = jnp.broadcast_to(jnp.sum(own, axis=1, keepdims=True), (8, 128))
                return carry

            lax.fori_loop(first, last, one, 0)

        def span(n, parts, f):
            cuts = [n * k // parts for k in range(parts + 1)]
            return [lambda a=a, b=b: f(a, b) for a, b in zip(cuts, cuts[1:])]

        fillers = span(HB, 8, round_c2)
        fillers += [finish_b, lambda: c2_copy.start(), lambda: all_sum_step(0, 0)]
        fillers += [lambda: q_copy.wait()] + span(CH, 8, order_q)
        fillers += [lambda: all_sum_step(0, 1), lambda: c2_copy.wait()] + span(CH // 2, 16, order_c2)
        fillers += [lambda: all_sum_step(0, 2)]
        waited = []

        def before_send(m):
            if not waited and m["hi"] > NT0:
                waited.append(1)
                c1_copy.wait()

        tree(g0, TT0, plan0, before_send=before_send, fillers=[(0, f) for f in fillers])
        tree_sent(g0, plan0)
        to_partner(arps.at[0], arpr.at[0], arp_sem.at[0, 0], arp_sem.at[0, 1]).wait()
        ap[...] = jnp.where(row < 4, arps[0] + arpr[0], arps[0])
        for t in range(NT):
            pv[t] = jnp.broadcast_to(ap[4 + t : 5 + t, :], (8, 128))

        def unpack(s, carry):
            chip_s = source_of(s)
            for g in range(G):
                for t in range(JW):
                    pair = g0[s * TT0 + g * JW + t].astype(F32)
                    kbuf[(chip_s * G + g) * JN + 2 * t] = pair[:8]
                    kbuf[(chip_s * G + g) * JN + 2 * t + 1] = pair[8:]
                for h in range(2):
                    pair = g0[s * TT0 + NT0 + h * G + g].astype(F32)
                    at = pl.ds(pl.multiple_of(chip_s * NR + g * 8, 8), 8)
                    c1f[at, 256 * h : 256 * h + 128] = pair[:8]
                    c1f[at, 256 * h + 128 : 256 * h + 256] = pair[8:]
            return carry

        lax.fori_loop(0, CH, unpack, 0)
        c1b[...] = c1f[...].astype(BF16)

        def finish_lp():
            lp[...] = jnp.concatenate([bp[...]] * NT, axis=1) - 2.0 * bacc[...]

        bacc[...] = jnp.zeros_like(bacc)
        JC = CK // 128

        def first_chunk(n, carry):
            cols = []
            for t in range(JC):
                tiles = [kbuf[g * JN + n * JC + t] for g in range(CH * G)]
                cols.append(jnp.concatenate(tiles, axis=0))
            plan_c = jnp.concatenate(cols, axis=1).astype(BF16)
            lead = jnp.dot(c1b[...], plan_c, preferred_element_type=F32).astype(BF16)
            c2c = jnp.concatenate([c2n[core * HB + n * JC + t] for t in range(JC)], axis=1)
            bacc[...] += lax.dot_general(c2c, lead, (((1,), (1,)), ((), ())), preferred_element_type=F32)
            return carry

        lax.fori_loop(0, KJ // CK, first_chunk, 0)
        finish_lp()

        def chunk(n, carry):
            at = pl.ds(pl.multiple_of(n * CK, CK), CK)
            lead = jnp.dot(tt[at, :], c1b[...], preferred_element_type=F32).astype(BF16)
            bacc[...] += jnp.dot(c2p[:, at], lead, preferred_element_type=F32)
            return carry

        def costs():
            copy = to_partner(lp.at[pl.ds(other * JB, JB)], lprecv, lp_sem.at[0], lp_sem.at[1])
            copy.start()
            copy.wait()
            own = lp[pl.ds(pl.multiple_of(core * JB, JB), JB), :] + lprecv[...]
            return own + jnp.concatenate([ap[t : t + 1, :] for t in range(NT)], axis=1)

        def block(s):
            return kbuf[pl.ds(s * TB, TB)].reshape(JT, NT, 8, 128)

        def weighted(kk, u):
            w = (kk[:, 0] * u[0] + kk[:, 1] * u[1]) + (kk[:, 2] * u[2] + kk[:, 3] * u[3])
            return jnp.sum(w, axis=2, keepdims=True)

        def passes(u, rescale=False, last=False):
            def one(g, buf):
                for k in range(GS):
                    s = g * GS + k
                    kk = block(s)
                    if rescale:
                        kk = kk * fb[:, pl.ds(s, 1), :][None]
                        kbuf[pl.ds(s * TB, TB)] = kk.reshape(TB, 8, 128)
                    cbuf[buf, k] = jnp.broadcast_to(weighted(kk, u), (JT, 8, 128))

            def two(g, buf, acc):
                for k in range(GS):
                    s = g * GS + k
                    v = qrep[s] / cbuf[buf, k]
                    kk = block(s)
                    if last:
                        vbuf[s] = v
                        t = (kk * u[None]) * v[:, None]
                        flat = jnp.concatenate([t[:, i].reshape(JB, 128) for i in range(NT)], axis=1)
                        tt[pl.ds(pl.multiple_of(s * JB, JB), JB), :] = flat.astype(BF16)
                    else:
                        acc = acc + jnp.sum(kk * v[:, None], axis=0)
                return acc

            def both(g, acc):
                acc = two(g - 1, lax.rem(g - 1, 2), acc)
                one(g, lax.rem(g, 2))
                return acc

            one(0, 0)
            acc = lax.fori_loop(1, NG, both, jnp.zeros((NT, 8, 128), F32))
            return two(NG - 1, (NG - 1) % 2, acc)

        def row_scale(acc, par):
            xs[par] = acc
            copy = to_partner(xs.at[par], xr.at[par], x_ssem.at[par], x_rsem.at[par])
            copy.start()
            copy.wait()
            total = jnp.sum(acc + xr[par], axis=1, keepdims=True)
            return pv[...] / jnp.broadcast_to(total, (NT, 8, 128))

        def outer(r, carry):
            scale = 1.4426950408889634 / eps_ref[r]
            cost = costs()
            for jt in range(JT):
                for t in range(NT):
                    land[jt * NT + t] = cost[jt * 8 : jt * 8 + 8, t * 128 : t * 128 + 128]

            def exps(s):
                ll = land[s * TB : s * TB + TB].reshape(JT, NT, 8, 128)
                low = jnp.min(jnp.min(ll, axis=0), axis=1, keepdims=True)
                kk = jnp.exp2((low[None] - ll) * scale)
                kbuf[s * TB : s * TB + TB] = kk.reshape(TB, 8, 128)
                mb[:, s : s + 1, :] = low
                sb[:, s : s + 1, :] = jnp.sum(jnp.sum(kk, axis=0), axis=1, keepdims=True)

            pl.semaphore_wait(credit, NL)
            tree(land, TB, plan, on_slot=exps, fillers=[(0, lambda: exps(0))])
            tree_sent(land, plan)
            give_credit()

            low = jnp.min(mb[...], axis=1, keepdims=True)
            part = jnp.sum(sb[...] * jnp.exp2((low - mb[...]) * scale), axis=1, keepdims=True)
            mss[0] = jnp.broadcast_to(low, (NT, 8, 128))
            mss[1] = jnp.broadcast_to(part, (NT, 8, 128))
            copy = to_partner(mss, msr, ms_sem.at[0], ms_sem.at[1])
            copy.start()
            copy.wait()
            least = jnp.minimum(mss[0], msr[0])
            total = mss[1] * jnp.exp2((least - mss[0]) * scale) + msr[1] * jnp.exp2((least - msr[0]) * scale)
            fb[...] = jnp.exp2((least[:, :1] - mb[...]) * scale)
            u = pv[...] / total

            u = row_scale(passes(u, rescale=True), 1)

            def sweep(t, u):
                return row_scale(passes(u), lax.rem(t, 2))

            u = lax.fori_loop(2, sweeps, sweep, u)
            passes(u, last=True)
            ub[...] = u
            bacc[...] = jnp.zeros_like(bacc)
            lax.fori_loop(0, KJ // CK, chunk, 0)
            finish_lp()
            return carry

        lax.fori_loop(0, steps, outer, 0)

        pl.semaphore_wait(credit, NL)
        cost = costs()
        plan_own = (block(0) * ub[...][None]) * vbuf[0][:, None]
        total = jnp.zeros((8, 128), F32)
        for jt in range(JT):
            for t in range(NT):
                total = total + cost[jt * 8 : jt * 8 + 8, t * 128 : t * 128 + 128] * plan_own[jt, t]
        ars[1, 0] = total
        all_sum_send(1, 0)

        it = lax.div(chip * NR, 128)
        inside = pl.multiple_of(lax.rem(chip * NR, 128), 8)

        def rows_of(s, carry):
            kk = jnp.concatenate([kbuf[s * TB + jt * NT + it] for jt in range(JT)], axis=0)
            uu = jnp.concatenate([ub[it]] * JT, axis=0)
            t = (kk * uu) * vbuf[s].reshape(JB, 128)
            none = jnp.zeros_like(t)
            both = jnp.where(core == 0, jnp.concatenate([t, none], axis=0), jnp.concatenate([none, t], axis=0))
            trb[...] = both.T
            obuf[source_of(s)] = trb[pl.ds(inside, NR), :]
            return carry

        lax.fori_loop(0, CH, rows_of, 0)
        o_copy = to_partner(obuf.at[pl.ds(other * HB, HB)], orecv, o_sem.at[0], o_sem.at[1])
        o_copy.start()
        all_sum_step(1, 0)
        o_copy.wait()
        for b in range(HB):
            out_ref[:, b * 128 : b * 128 + 128] = obuf[core * HB + b] + orecv[b]
        all_sum_step(1, 1)
        all_sum_step(1, 2)
        to_partner(arps.at[1], arpr.at[1], arp_sem.at[1, 0], arp_sem.at[1, 1]).wait()
        loss_ref[0] = jnp.sum(arps[1] + arpr[1])

    vm = pltpu.VMEM
    dma = pltpu.SemaphoreType.DMA
    scratch = [
        vm((CH * TB, 8, 128), F32),
        vm((CH * TB, 8, 128), F32),
        vm((CH * TT0, 16, 128), BF16),
        vm((KJ, n_rows), BF16),
        vm((n_rows, n_rows), F32),
        vm((n_rows, n_rows), BF16),
        vm((CH, 128, 128), BF16),
        vm((128, KJ), BF16),
        vm((128, n_rows), F32),
        vm((128, n_rows), F32),
        vm((JB, n_rows), F32),
        vm((128, 128), F32),
        vm((CH, 128), F32),
        vm((CH, JT, 8, 128), F32),
        vm((CH, JT, 8, 128), F32),
        vm((2, GS, JT, 8, 128), F32),
        vm((NT, CH, 128), F32),
        vm((NT, CH, 128), F32),
        vm((NT, CH, 128), F32),
        vm((NT, 8, 128), F32),
        vm((8, 128), F32),
        vm((2, NT, 8, 128), F32),
        vm((2, NT, 8, 128), F32),
        vm((2, NT, 8, 128), F32),
        vm((2, NT, 8, 128), F32),
        vm((NT, 8, 128), F32),
        vm((2, 3, 8, 128), F32),
        vm((2, 3, 3, 8, 128), F32),
        vm((2, 8, 128), F32),
        vm((2, 8, 128), F32),
        vm((CH, NR, 128), F32),
        vm((HB, NR, 128), F32),
        vm((128, 128), F32),
        dma((NL,)),
        dma((max(len(plan["msgs"]), len(plan0["msgs"])),)),
        pltpu.SemaphoreType.REGULAR,
        dma((2,)),
        dma((2,)),
        dma((2,)),
        dma((2,)),
        dma((2,)),
        dma((2,)),
        dma((2,)),
        dma((2, 3, 3)),
        dma((2, 3, 3)),
        dma((2, 2)),
        dma((2,)),
    ]
    return kernel, scratch


def solution(mesh):
    chips = mesh.shape["rows"]
    dims = torus_of(chips)
    grid_spec = P(("pairs", "rows"), "cols")

    def local_fn(c1, c2, t0, p, q, eps):
        n_rows, n_cols = p.shape[0] * chips, q.shape[0] * mesh.shape["cols"]
        kernel, scratch = make_kernel(dims, n_rows, n_cols, eps.shape[0], SWEEPS)
        vmem = pl.BlockSpec(memory_space=pltpu.VMEM)
        smem = pl.BlockSpec(memory_space=pltpu.SMEM)
        return pl.pallas_call(
            kernel,
            name="gromov",
            out_shape=(jax.ShapeDtypeStruct(t0.shape, F32), jax.ShapeDtypeStruct((1,), F32)),
            in_specs=[smem, smem, vmem, vmem, vmem, vmem],
            out_specs=(vmem, smem),
            scratch_shapes=scratch,
            compiler_params=pltpu.CompilerParams(
                collective_id=0, has_side_effects=True, vmem_limit_bytes=60 * 1024 * 1024
            ),
        )(eps, p, c1, c2, t0, q.reshape(chips // 2, 128))

    return jax.shard_map(
        local_fn,
        mesh=mesh,
        in_specs=(grid_spec, grid_spec, grid_spec, P(("pairs", "rows")), P(("pairs", "cols")), P("pairs")),
        out_specs=(grid_spec, P("pairs")),
        check_vma=False,
    )
```

time: 21700 us -> 519 us (0.02)
  blocking collectives: 20800 us -> 0 us
  waiting for transfers between devices: 690 us -> 0 us
  Pallas kernels: 0 us -> 515 us
    psum x123 -> x0, blocking collectives: 20700 us -> none  [the longest x60 17200 us: sweep(): lax.psum(jnp.sum(kernel * row_scale[:, None], axis=0), 'rows')]
    all_gather x8 -> x0, waiting for transfers between devices: 690 us -> none  [the longest x7 690 us: cost_of(): lax.all_gather(plan_blk.astype(jnp.bfloat16), 'rows', axis=0, tiled=True)]
    pallas_call x0 -> x1, Pallas kernels: none -> 515 us  [local_fn(): pl.pallas_call(kernel, name='gromov', out_shape=(jax.ShapeDtypeStruct(t0....]
  transfers between devices with their start and end apart: 8 -> 0, of which waited for: 6 -> 0; matrix products, arithmetic and copies ran while one was open for 0% -> 0% of each run, Pallas kernels for 0% -> 0%
where the time goes in v1:
time: 519 us
  Pallas kernels  515 us (99%)
    pallas_call x1, Pallas kernels, local_fn(): pl.pallas_call(kernel, name='gromov', out_shape=(jax.ShapeDtypeStruct(t0....  515 us

profile of v1, /device:TPU:1, one launch (start us, length us, event | category | flops | bytes accessed | tf_op | source)
XLA Modules:
  0.0 519.3 jit_solution(15427277847283240099)
XLA Ops:
  0.6 515.3 %gromov.1 = (f32[8,4096]{1,0:T(8,128)}, f32[1]{0:T(128)}) custom-call(f32[6]{0:T(128)} %eps_ref.1, f32[8]{0:T(128)} %p_ref.1, f32[8,256]{1,0:T(8,128)} %c1_ref.1, f32[128,4096]{1,0:T(8,128)} %c2_ref.1, f32[8,4096]{1,0:T(8,128)} %t0_ref.1, f32[32,128]{1,0:T(8,128)} %bitcast.1), custom_call_target="tpu_custom_call" | custom-call | tf_op jit(solution)/shard_map/gromov/pallas_call | solution.py:564
  515.9 1.6 copy.10

commit v2 on v1

--- a/solution.py
+++ b/solution.py
@@ -107,7 +107,7 @@
     TT0 = NT0 + 2 * G
     KJ = CH * JB
     CK = min(512, KJ)
-    GS = min(8, CH // 2)
+    GS = min(4, CH // 2)
     NG = CH // GS
     assert NT == 4 and n_cols == CH * 128 and JN == HB
     plan0 = tree_plan(dims, TT0, 4096 / 46.6e3)
@@ -382,12 +382,12 @@
                     if rescale:
                         kk = kk * fb[:, pl.ds(s, 1), :][None]
                         kbuf[pl.ds(s * TB, TB)] = kk.reshape(TB, 8, 128)
-                    cbuf[buf, k] = jnp.broadcast_to(weighted(kk, u), (JT, 8, 128))
+                    cbuf[buf, k] = qrep[s] / jnp.broadcast_to(weighted(kk, u), (JT, 8, 128))
 
             def two(g, buf, acc):
                 for k in range(GS):
                     s = g * GS + k
-                    v = qrep[s] / cbuf[buf, k]
+                    v = cbuf[buf, k]
                     kk = block(s)
                     if last:
                         vbuf[s] = v
@@ -398,13 +398,17 @@
                         acc = acc + jnp.sum(kk * v[:, None], axis=0)
                 return acc
 
-            def both(g, acc):
-                acc = two(g - 1, lax.rem(g - 1, 2), acc)
-                one(g, lax.rem(g, 2))
-                return acc
+            def both(n, acc):
+                one(2 * n + 1, 1)
+                acc = two(2 * n, 0, acc)
+                one(2 * n + 2, 0)
+                return two(2 * n + 1, 1, acc)
 
             one(0, 0)
-            acc = lax.fori_loop(1, NG, both, jnp.zeros((NT, 8, 128), F32))
+            acc = lax.fori_loop(0, (NG - 1) // 2, both, jnp.zeros((NT, 8, 128), F32))
+            if NG % 2 == 0:
+                one(NG - 1, 1)
+                acc = two(NG - 2, 0, acc)
             return two(NG - 1, (NG - 1) % 2, acc)
 
         def row_scale(acc, par):

time: 519 us -> 479 us (0.923)
  Pallas kernels: 515 us -> 475 us
    pallas_call x1, Pallas kernels: 515 us -> 475 us  [local_fn(): pl.pallas_call(kernel, name='gromov', out_shape=(jax.ShapeDtypeStruct(t0....]
where the time goes in v2:
time: 479 us
  Pallas kernels  475 us (99%)
    pallas_call x1, Pallas kernels, local_fn(): pl.pallas_call(kernel, name='gromov', out_shape=(jax.ShapeDtypeStruct(t0....  475 us

profile of v2, /device:TPU:1, one launch (start us, length us, event | category | flops | bytes accessed | tf_op | source)
XLA Modules:
  0.0 478.9 jit_solution(2453339623408173070)
XLA Ops:
  0.6 474.8 %gromov.1 = (f32[8,4096]{1,0:T(8,128)}, f32[1]{0:T(128)}) custom-call(f32[6]{0:T(128)} %eps_ref.1, f32[8]{0:T(128)} %p_ref.1, f32[8,256]{1,0:T(8,128)} %c1_ref.1, f32[128,4096]{1,0:T(8,128)} %c2_ref.1, f32[8,4096]{1,0:T(8,128)} %t0_ref.1, f32[32,128]{1,0:T(8,128)} %bitcast.1), custom_call_target="tpu_custom_call" | custom-call | tf_op jit(solution)/shard_map/gromov/pallas_call | solution.py:568
  475.5 1.6 copy.10
